TPU v7x, 32 devices: a whole 2x2x4 slice. The times are simulated.
32 devices in a mesh: tab: 8 (over y, x, core), rep: 4 (over z).
Axes of the slice: x: 2, y: 2, z: 4, core: 2. Of those that a mesh axis runs over, the one named last changes fastest.
Arguments:
- pooled: bfloat16 [64, 4096, 128], P('tab', 'rep'), may hold values from -6 to 6
- widths: int32 [64], replicated, may hold values from 16 to 128, as said below
- placement: int32 [64], replicated, may hold values from 0 to 63, each once
- route: int32 [4, 1024], P('rep'), may hold values from 0 to 1023, each once within a row
- labels: int32 [4, 1024], P('rep'), may hold values 0 or 1
- proj: bfloat16 [64, 128, 32], replicated, may hold values from -0.5 to 0.5
- senet_in: float32 [64, 32], replicated, may hold values from -6 to 6
- senet_out: float32 [32, 64], replicated, may hold values from -1 to 1
- bilinear: float32 [32, 32], replicated, may hold values from -1 to 1
- w_first: bfloat16 [4096, 256], replicated, may hold values from -0.09375 to 0.09375
- w_second: bfloat16 [256, 256], replicated, may hold values from -0.75 to 0.75
- w_last: bfloat16 [256], replicated, may hold values from -0.375 to 0.375
Outputs:
- scores: float32 [4, 1024], P('rep', 'tab')
- d_pooled: bfloat16 [64, 4096, 128], P('tab', 'rep')
- d_proj: float32 [64, 128, 32], P('tab')
- d_senet_in: float32 [64, 32], replicated
- d_senet_out: float32 [32, 64], replicated
- d_bilinear: float32 [32, 32], replicated
- d_first: float32 [4096, 256], P('tab')
- d_second: float32 [256, 256], replicated
- d_last: float32 [256], replicated
Inputs may be any that keep to these rules, and one draw needn't show every extreme that they name: `widths`: each field's width is 128, 64, 32 or 16. `placement`: a permutation of the fields. `route`: each row is a permutation of 0 to 1023.
All inputs are finite; a program needn't handle non-finite values. No bound on the sum of `labels` on one device may be relied on, other than what follows from the above.
Results may differ from a plain program's by a relative error of at most 0.017.
Values may be sent and summed in bfloat16 or wider, within the bound.
No kernel may reach another device: no remote copies, remote signals or barrier semaphores. Data moves between devices by JAX's collectives and lax.ppermute only.
A program may use at most 64 MiB of HBM per device.

v0:
```python
import jax
import jax.numpy as jnp
from jax import lax
from jax.sharding import PartitionSpec as P

PRECISE = lax.Precision.HIGHEST


def silu_slope(pre_act):
    logistic = jax.nn.sigmoid(pre_act)
    return logistic * (1.0 + pre_act * (1.0 - logistic))


def bilinear_forward(fields_in, bilinear, factor):
    product = jnp.einsum("fnc,cd->fnd", fields_in, bilinear, precision=PRECISE)
    others = jnp.sum(fields_in, axis=0, keepdims=True) - fields_in
    return (product * others * factor, product, others)


def bilinear_backward(fields_in, product, others, upstream, bilinear, factor):
    d_product = upstream * others * factor
    d_others = upstream * product * factor
    d_fields = jnp.einsum("fnd,cd->fnc", d_product, bilinear, precision=PRECISE)
    d_fields = d_fields + jnp.sum(d_others, axis=0, keepdims=True) - d_others
    d_weight = jnp.einsum("fnc,fnd->cd", fields_in, d_product, precision=PRECISE)
    return (d_fields, d_weight)


def owner_pass(embeds, targets, senet_in, senet_out, bilinear, w_first, w_second, w_last):
    count = embeds.shape[0]
    width = embeds.shape[2]
    hidden = w_second.shape[0]
    factor = count ** (-0.5)
    first = w_first.reshape(2, count, width, hidden)
    dense = embeds.astype(jnp.float32)
    squeeze = jnp.mean(dense, axis=2)
    pre_one = jnp.einsum("fn,fr->rn", squeeze, senet_in, precision=PRECISE)
    act_one = jax.nn.silu(pre_one)
    pre_two = jnp.einsum("rn,rf->fn", act_one, senet_out, precision=PRECISE)
    weights = jax.nn.sigmoid(pre_two)
    scaled = weights[:, :, None] * dense
    plain_out, plain_prod, plain_rest = bilinear_forward(dense, bilinear, factor)
    scaled_out, scaled_prod, scaled_rest = bilinear_forward(scaled, bilinear, factor)
    joined = jnp.stack([plain_out, scaled_out]).astype(jnp.bfloat16)
    pre_hidden = jnp.einsum("kfnc,kfch->nh", joined, first, preferred_element_type=jnp.float32)
    hidden_one = jax.nn.silu(pre_hidden).astype(jnp.bfloat16)
    pre_second = jnp.dot(hidden_one, w_second, preferred_element_type=jnp.float32)
    hidden_two = jax.nn.silu(pre_second).astype(jnp.bfloat16)
    logits = jnp.dot(hidden_two, w_last, preferred_element_type=jnp.float32)
    grad_logit = jax.nn.sigmoid(logits) - targets
    d_last = jnp.dot(grad_logit, hidden_two.astype(jnp.float32), precision=PRECISE)
    last_wide = w_last.astype(jnp.float32)
    d_pre_two = (grad_logit[:, None] * last_wide[None, :] * silu_slope(pre_second)).astype(
        jnp.bfloat16
    )
    d_second = jnp.dot(hidden_one.T, d_pre_two, preferred_element_type=jnp.float32)
    back_two = jnp.dot(d_pre_two, w_second.T, preferred_element_type=jnp.float32)
    d_pre_one = (back_two * silu_slope(pre_hidden)).astype(jnp.bfloat16)
    d_first = jnp.einsum(
        "kfnc,nh->kfch", joined, d_pre_one, preferred_element_type=jnp.float32
    ).reshape(-1, hidden)
    d_joined = jnp.einsum("nh,kfch->kfnc", d_pre_one, first, preferred_element_type=jnp.float32)
    d_plain, d_bil_plain = bilinear_backward(
        dense, plain_prod, plain_rest, d_joined[0], bilinear, factor
    )
    d_scaled, d_bil_scaled = bilinear_backward(
        scaled, scaled_prod, scaled_rest, d_joined[1], bilinear, factor
    )
    d_weights = jnp.sum(d_scaled * dense, axis=2)
    d_pre_w = d_weights * weights * (1.0 - weights)
    d_senet_out = jnp.einsum("rn,fn->rf", act_one, d_pre_w, precision=PRECISE)
    d_act = jnp.einsum("fn,rf->rn", d_pre_w, senet_out, precision=PRECISE) * silu_slope(pre_one)
    d_senet_in = jnp.einsum("fn,rn->fr", squeeze, d_act, precision=PRECISE)
    d_squeeze = jnp.einsum("rn,fr->fn", d_act, senet_in, precision=PRECISE)
    d_embeds = d_plain + weights[:, :, None] * d_scaled + d_squeeze[:, :, None] / width
    small = (d_senet_in, d_senet_out, d_bil_plain + d_bil_scaled, d_second, d_last)
    return (logits, d_embeds.astype(jnp.bfloat16), small, d_first, joined, d_pre_one)


def shards(
    pooled,
    widths,
    placement,
    route,
    labels,
    proj,
    senet_in,
    senet_out,
    bilinear,
    w_first,
    w_second,
    w_last,
):
    tab_count = lax.axis_size("tab")
    tab_index = lax.axis_index("tab")
    local_count = pooled.shape[0]
    rep_rows = pooled.shape[1]
    padded = pooled.shape[2]
    field_count = placement.shape[0]
    owner_rows = rep_rows // tab_count
    field_ids = jnp.arange(field_count, dtype=jnp.int32)
    matches = placement[:, None] == field_ids[None, :]
    slot_width = jnp.sum(jnp.where(matches, widths[None, :], 0), axis=1)
    slot_mask = (jnp.arange(padded, dtype=jnp.int32)[None, :] < slot_width[:, None]).astype(
        jnp.bfloat16
    )
    inverse = jnp.zeros_like(placement).at[placement].set(field_ids)
    targets = lax.dynamic_slice_in_dim(labels[0], tab_index * owner_rows, owner_rows).astype(
        jnp.float32
    )
    first_slot = tab_index * local_count
    local_fields = lax.dynamic_slice_in_dim(placement, first_slot, local_count)
    local_mask = lax.dynamic_slice_in_dim(slot_mask, first_slot, local_count, 0)
    local_proj = jnp.take(proj, local_fields, axis=0)
    masked = pooled * local_mask[:, None, :]
    embed_local = jnp.einsum(
        "fnc,fcd->fnd", masked, local_proj, preferred_element_type=jnp.float32
    ).astype(jnp.bfloat16)
    embed_slot = lax.all_to_all(embed_local, "tab", split_axis=1, concat_axis=0, tiled=True)
    logits, d_embeds, small, d_first_part, joined, d_pre_one = owner_pass(
        embed_slot[inverse], targets, senet_in, senet_out, bilinear, w_first, w_second, w_last
    )
    d_slot = d_embeds[placement]
    d_local = lax.all_to_all(d_slot, "tab", split_axis=0, concat_axis=1, tiled=True)
    back = jnp.einsum("fnd,fcd->fnc", d_local, local_proj, preferred_element_type=jnp.float32)
    back = (back * local_mask[:, None, :]).astype(jnp.bfloat16)
    d_proj_part = jnp.einsum("fnc,fnd->fcd", masked, d_local, preferred_element_type=jnp.float32)
    d_proj = lax.psum(d_proj_part.astype(jnp.bfloat16), "rep").astype(jnp.float32)
    first_all = lax.psum_scatter(d_first_part, ("tab", "rep"), scatter_dimension=0, tiled=True)
    d_first = lax.all_gather(first_all.astype(jnp.bfloat16), "rep", axis=0, tiled=True).astype(
        first_all.dtype
    )
    part_in, part_out, part_bil, part_second, part_last = small
    d_senet_in, d_senet_out, d_bilinear, d_second, d_last = lax.psum(
        (part_in, part_out, part_bil, part_second, part_last), ("tab", "rep")
    )
    all_logits = lax.all_gather(logits, "tab", axis=0, tiled=True)
    wanted = lax.dynamic_slice_in_dim(route[0], tab_index * owner_rows, owner_rows)
    scores = jnp.take(all_logits, wanted)[None, :]
    return (scores, back, d_proj, d_senet_in, d_senet_out, d_bilinear, d_first, d_second, d_last)


def solution(mesh):
    placed = (
        P("tab", "rep", None),
        P(),
        P(),
        P("rep", None),
        P("rep", None),
        P(),
        P(),
        P(),
        P(),
        P(),
        P(),
        P(),
    )
    return jax.shard_map(
        shards,
        mesh=mesh,
        in_specs=placed,
        out_specs=(
            P("rep", "tab"),
            P("tab", "rep", None),
            P("tab", None, None),
            P(),
            P(),
            P(),
            P("tab", None),
            P(),
            P(),
        ),
        check_vma=False,
    )
```

profile of v0, /device:TPU:0, one launch (start us, length us, event | category | flops | bytes accessed | tf_op | source)
XLA Modules:
  0.0 254.4 jit_solution(10931208529390182150)
XLA Ops:
  8.0 1.0 select_reduce_fusion
  9.0 0.7 compare_and_fusion
  9.8 0.1 dynamic-slice.2
  9.9 0.1 fusion.91
  9.9 1.6 gather_fusion
  11.5 2.4 fusion.15
  14.0 2.5 copy.54
  16.5 4.6 %reshape.143 = bf16[8,2,16384]{2,1,0:T(2,128)(2,1)} reshape(bf16[1024,8,32]{2,1,0:T(8,128)(2,1)} %bitcast.132) | data formatting | bytes 1048576
  21.0 5.2 %all-to-all-start = ((bf16[8,2,16384]{2,1,0:T(2,128)(2,1)}), bf16[8,2,16384]{2,1,0:T(2,128)(2,1)S(1)}, u32[]{:S(2)}, u32[]{:S(2)}) async-start(bf16[8,2,16384]{2,1,0:T(2,128)(2,1)} %reshape.143), calls=%async_computation | async-start | bytes 1048576 | tf_op jit(solution)/shard_map/all_to_all | solution.py:119
  26.2 0.0 all-reduce.4.cloned.1.call-start
  26.3 1.0 scatter_custom_fusion
  27.3 8.6 %all-to-all-done = bf16[8,2,16384]{2,1,0:T(2,128)(2,1)S(1)} async-done(((bf16[8,2,16384]{2,1,0:T(2,128)(2,1)}), bf16[8,2,16384]{2,1,0:T(2,128)(2,1)S(1)}, u32[]{:S(2)}, u32[]{:S(2)}) %all-to-all-start) | async-done | bytes 524320 | tf_op jit(solution)/shard_map/all_to_all | solution.py:119
  35.9 2.0 reshape.144
  37.9 2.2 copy.56
  40.2 0.7 gather_fusion.1
  40.8 0.1 convert_reduce_fusion
  41.0 0.1 convolution_bitcast_fusion.3
  41.1 0.2 fusion.34
  41.4 0.2 convert_reduce_fusion.1
  41.6 1.1 fusion.9
  42.7 0.6 fusion.77
  43.3 0.4 fusion.52
  43.8 0.5 fusion.22
  44.3 0.2 copy-done.2
  44.5 0.2 copy-done.3
  44.7 0.1 copy-done.13
  44.8 0.2 multiply_convert_fusion.2
  45.0 0.8 divide_subtract_fusion
  45.9 0.2 fusion.29
  46.1 0.7 convolution_bitcast_fusion
  46.9 0.5 fusion.69
  47.4 1.5 fusion.44
  49.0 0.1 fusion.36
  49.1 0.2 fusion.30
  49.4 1.5 fusion.14
  50.8 1.4 gather_fusion.3
  52.3 13.1 %all_to_all.36 = bf16[64,128,32]{1,2,0:T(8,128)(2,1)S(1)} all-to-all(bf16[64,128,32]{1,2,0:T(8,128)(2,1)} %gather_fusion.3), channel_id=1, replica_groups=mesh['tab'=8,'rep'=4] {'tab'}, dimensions={0} | all-to-all | bytes 1048576 | tf_op jit(solution)/shard_map/all_to_all | solution.py:124
  65.4 2.9 %fusion.25 = bf16[8,128,32]{1,2,0:T(8,128)(2,1)} fusion(bf16[8,1024,128]{2,1,0:T(8,128)(2,1)} %param.12, bf16[8,128]{1,0:T(8,128)(2,1)S(1)} %copy-done.11, bf16[8,8,4,8,128]{4,3,2,1,0:T(8,128)(2,1)S(1)} %bitcast.134), kind=kOutput, calls=%fused_computation.36 | convolution fusion | flops 71335936 | bytes 2689024 | tf_op jit(solution)/shard_map/fnc,fnd->fcd/dot_general | solution.py:127
  68.2 0.0 all-reduce.4.cloned.1.call-update
  68.3 0.0 reduce-scatter.2.cloned.1.call-start
  68.3 3.8 %fusion.107 = f32[2,64,32,256]{3,2,1,0:T(8,128)} fusion(bf16[128,256,1,1]{1,0,3,2:T(8,128)(2,1)S(1)} %fusion.29, bf16[1,64,128,32]{2,3,1,0:T(8,128)(2,1)} %copy-done.3, bf16[1,64,128,32]{2,3,1,0:T(8,128)(2,1)} %copy-done.2), kind=kOutput, calls=%fused_computation.145 | convolution fusion | flops 268959744 | bytes 5308416 | tf_op jit(solution)/shard_map/kfnc,nh->kfch/dot_general | solution.py:59
  72.2 0.0 reduce-scatter.2.cloned.1.call-update
  72.2 0.0 all-reduce.6.cloned.1.call-start
  72.2 0.7 fusion.86
  72.9 8.0 %all-gather = f32[8,1,128]{2,1,0:T(1,128)S(1)} all-gather(f32[1,1,128]{2,1,0:T(1,128)S(1)} %bitcast.137), channel_id=1, replica_groups=mesh['tab'=8,'rep'=4] {'tab'}, dimensions={0}, use_global_device_ids=true | all-gather | bytes 4608 | tf_op jit(solution)/shard_map/all_gather | solution.py:137
  80.9 1.0 gather_fusion.2
  81.9 2.0 convolution_bitcast_fusion.1
  84.0 1.2 and_select_fusion
  85.2 0.2 fusion.71
  85.3 0.1 fusion.87
  85.5 0.2 fusion.82
  85.6 0.0 copy-done.16
  85.7 1.0 fusion.105
  86.6 2.4 fusion.37
  89.1 0.0 all-reduce.6.cloned.1.call-update
  89.1 41.4 %all-reduce = (f32[64,32]{0,1:T(8,128)}, f32[32,64]{1,0:T(8,128)}, f32[32,32]{1,0:T(8,128)}, f32[256]{0:T(256)}) all-reduce(f32[64,32]{0,1:T(8,128)S(1)} %fusion.71, f32[32,64]{1,0:T(8,128)S(1)} %fusion.82, f32[32,32]{1,0:T(8,128)S(1)} %fusion.37, f32[256]{0:T(256)S(1)} %bitcast.136), channel_id=1, replica_groups=mesh['tab'=8,'rep'=4] {'tab','rep'}, use_global_device_ids=true, to_apply=%region_9.10 | all-reduce | flops 5376 | bytes 43008 | tf_op jit(solution)/shard_map/psum | solution.py:134
  130.5 2.2 multiply_convert_fusion
  132.7 1.5 convert_element_type.68
  134.2 87.1 %reduce-scatter.2.cloned.1.call-done = f32[128,256]{1,0:T(8,128)} async-done(((f32[4096,256]{1,0:T(8,128)}), f32[128,256]{1,0:T(8,128)}) %reduce-scatter.2.cloned.1.call-update) | async-done | bytes 131088 | tf_op jit(solution)/shard_map/reduce_scatter | solution.py:129
  221.3 0.9 convert_element_type.69
  222.2 14.3 %all_gather.7 = bf16[512,256]{1,0:T(8,128)(2,1)S(1)} all-gather(bf16[128,256]{1,0:T(8,128)(2,1)S(1)} %convert_element_type.69), channel_id=1, replica_groups=mesh['tab'=8,'rep'=4] {'rep'}, dimensions={0}, use_global_device_ids=true | all-gather | bytes 327680 | tf_op jit(solution)/shard_map/all_gather | solution.py:130
  236.5 0.8 convert_element_type.70
  237.3 8.0 %all-reduce.6.cloned.1.call-done = f32[256,256]{1,0:T(8,128)} async-done(((f32[256,256]{1,0:T(8,128)}), f32[256,256]{1,0:T(8,128)}) %all-reduce.6.cloned.1.call-update) | async-done | bytes 262160 | tf_op jit(solution)/shard_map/psum | solution.py:134
  245.3 1.7 copy.91
  (48 shorter events, 0.2 us)
Async XLA Ops:
  8.0 35.7 %copy-start = (bf16[4096,256]{1,0:T(8,128)(2,1)S(1)}, bf16[4096,256]{1,0:T(8,128)(2,1)}, u32[]{:S(2)}) copy-start(bf16[4096,256]{1,0:T(8,128)(2,1)} %param.21) | copy-start | bytes 6291460
  9.8 6.7 %copy-start.8 = (pred[8]{0:T(512)(128)(4,1)}, pred[8]{0:T(512)(128)(4,1)S(1)}, u32[]{:S(2)}) copy-start(pred[8]{0:T(512)(128)(4,1)S(1)} %get-tuple-element.17) | copy-start | bytes 28
  9.9 6.5 %copy-start.10 = (bf16[8,128]{1,0:T(8,128)(2,1)}, bf16[8,128]{1,0:T(8,128)(2,1)S(1)}, u32[]{:S(2)}) copy-start(bf16[8,128]{1,0:T(8,128)(2,1)S(1)} %get-tuple-element.22) | copy-start | bytes 6148
  16.5 9.8 %copy-start.12 = (s32[64]{0:T(128)S(1)}, s32[64]{0:T(128)}, u32[]{:S(2)}) copy-start(s32[64]{0:T(128)} %param.14) | copy-start | bytes 772
  16.5 9.8 %copy-start.14 = (bf16[256]{0:T(256)(128)(2,1)S(1)}, bf16[256]{0:T(256)(128)(2,1)}, u32[]{:S(2)}) copy-start(bf16[256]{0:T(256)(128)(2,1)} %param.23) | copy-start | bytes 1540
  21.0 14.9 %all-to-all-start = ((bf16[8,2,16384]{2,1,0:T(2,128)(2,1)}), bf16[8,2,16384]{2,1,0:T(2,128)(2,1)S(1)}, u32[]{:S(2)}, u32[]{:S(2)}) async-start(bf16[8,2,16384]{2,1,0:T(2,128)(2,1)} %reshape.143), calls=%async_computation | async-start | bytes 1048576 | tf_op jit(solution)/shard_map/all_to_all | solution.py:119
  26.2 106.5 %all-reduce.4.cloned.1.call-start = ((), (), s32[]{:S(2)}) async-start(), calls=%async_computation.3 | async-start | bytes 131072 | tf_op jit(solution)/shard_map/psum | solution.py:128
  26.3 19.6 %copy-start.15 = (f32[256]{0:T(256)}, f32[256]{0:T(256)S(1)}, u32[]{:S(2)}) copy-start(f32[256]{0:T(256)S(1)} %convert_element_type.61) | copy-start | bytes 3076
  40.1 0.8 copy-start.5
  40.1 1.0 copy-start.6
  40.2 1.4 copy-start.4
  43.7 0.8 copy-start.2
  43.7 1.0 copy-start.3
  43.7 1.1 copy-start.13
  44.8 2.0 copy-start.17
  45.0 1.8 copy-start.19
  46.9 2.5 copy-start.1
  47.4 1.5 copy-start.7
  50.8 14.5 %copy-start.11 = (bf16[8,128]{1,0:T(8,128)(2,1)S(1)}, bf16[8,128]{1,0:T(8,128)(2,1)}, u32[]{:S(2)}) copy-start(bf16[8,128]{1,0:T(8,128)(2,1)} %copy-done.10) | copy-start | bytes 6148
  68.3 153.0 %reduce-scatter.2.cloned.1.call-start = ((), (), s32[]{:S(2)}) async-start(), calls=%async_computation.4 | async-start | bytes 4325376 | tf_op jit(solution)/shard_map/reduce_scatter | solution.py:129
  72.2 13.5 %copy-start.16 = (f32[256]{0:T(256)S(1)}, f32[256]{0:T(256)}, u32[]{:S(2)}) copy-start(f32[256]{0:T(256)} %copy-done.15) | copy-start | bytes 3076
  72.2 173.1 %all-reduce.6.cloned.1.call-start = ((), (), s32[]{:S(2)}) async-start(), calls=%async_computation.5 | async-start | bytes 524288 | tf_op jit(solution)/shard_map/psum | solution.py:134
  81.9 3.8 %copy-start.18 = (f32[128,256]{1,0:T(8,128)S(1)}, f32[128,256]{1,0:T(8,128)}, u32[]{:S(2)}) copy-start(f32[128,256]{1,0:T(8,128)} %copy-done.17) | copy-start | bytes 393220
  81.9 3.7 %copy-start.20 = (f32[128,256]{1,0:T(8,128)S(1)}, f32[128,256]{1,0:T(8,128)}, u32[]{:S(2)}) copy-start(f32[128,256]{1,0:T(8,128)} %copy-done.19) | copy-start | bytes 393220
  84.0 46.6 %copy-start.9 = (pred[8]{0:T(512)(128)(4,1)S(1)}, pred[8]{0:T(512)(128)(4,1)}, u32[]{:S(2)}) copy-start(pred[8]{0:T(512)(128)(4,1)} %copy-done.8) | copy-start | bytes 28
Sparse Core Ops, SparseCore 0:
  68.4 37.1 all-reduce.3
  111.7 133.5 all-reduce.5
Sparse Core Ops, SparseCore 1:
  72.3 149.0 reduce-scatter.1
where the time goes:
time: 255 us; the launch traced here: 254 us
  waiting for transfers between devices  104 us (41%)
  blocking collectives  76.9 us (30%)
  matrix products  25.2 us (10%)
  local copies, waits for them, and re-layouts  19.2 us (8%)
  between operations  16 us (6%)
  other arithmetic  8.18 us (3%)
  starting transfers between devices  5.32 us (2%)
    reduce_scatter x1, waiting for transfers between devices, shards(): lax.psum_scatter(d_first_part, ('tab', 'rep'), scatter_dimension=0, tiled...  87.1 us
    psum x1, blocking collectives, shards(): lax.psum((part_in, part_out, part_bil, part_second, part_last), ('tab', '...  41.4 us
    all_gather x1, blocking collectives, shards(): lax.all_gather(first_all.astype(jnp.bfloat16), 'rep', axis=0, tiled=True)  14.3 us
    all_to_all x1, blocking collectives, shards(): lax.all_to_all(d_slot, 'tab', split_axis=0, concat_axis=1, tiled=True)  13.1 us
    unnamed x46, local copies, waits for them, and re-layouts  8.85 us
    all_to_all x1, waiting for transfers between devices, shards(): lax.all_to_all(embed_local, 'tab', split_axis=1, concat_axis=0, tiled=True)  8.59 us
    all_gather x1, blocking collectives, shards(): all_logits = lax.all_gather(logits, 'tab', axis=0, tiled=True)  8.03 us
    psum x1, waiting for transfers between devices, shards(): lax.psum((part_in, part_out, part_bil, part_second, part_last), ('tab', '...  7.97 us
  transfers between devices with their start and end apart: 4, of which 3 were waited for; matrix products, arithmetic and copies ran while one was open for 7% of the time, Pallas kernels for 0%

commit v1 on v0

--- a/solution.py
+++ b/solution.py
@@ -116,7 +116,19 @@
     embed_local = jnp.einsum(
         "fnc,fcd->fnd", masked, local_proj, preferred_element_type=jnp.float32
     ).astype(jnp.bfloat16)
-    embed_slot = lax.all_to_all(embed_local, "tab", split_axis=1, concat_axis=0, tiled=True)
+    upper, top = (lax.axis_size("tab"), lax.axis_index("tab"))
+    response = embed_local.shape[1] // upper
+    main = jnp.roll(embed_local, -top * response, 1)
+    table = [lax.slice_in_dim(main, 0, response, axis=1)]
+    for num in range(1, upper):
+        mat_out = lax.slice_in_dim(main, num * response, (num + 1) * response, axis=1)
+        table.append(
+            lax.ppermute(
+                mat_out, axis_name="tab", perm=[(u, (u + num) % upper) for u in range(upper)]
+            )
+        )
+    v_next = jnp.concatenate(table[::-1], 0)
+    embed_slot = jnp.roll(v_next, (top + 1) * table[0].shape[0], 0)
     logits, d_embeds, small, d_first_part, joined, d_pre_one = owner_pass(
         embed_slot[inverse], targets, senet_in, senet_out, bilinear, w_first, w_second, w_last
     )

time: 255 us -> 246 us (0.965)
  local copies, waits for them, and re-layouts: 19.2 us -> 8.72 us
  starting transfers between devices: 5.32 us -> 8.48 us
  waiting for transfers between devices: 104 us -> 101 us
    all_to_all x1 -> x0, waiting for transfers between devices: 8.59 us -> none  [shards(): lax.all_to_all(embed_local, 'tab', split_axis=1, concat_axis=0, tiled=True)]
    ppermute x0 -> x7, starting transfers between devices: none -> 8.36 us  [shards(): lax.ppermute(mat_out, axis_name='tab', perm=[(u, (u + num) % upper) for u...]
    ppermute x0 -> x7, waiting for transfers between devices: none -> 6.78 us  [shards(): lax.ppermute(mat_out, axis_name='tab', perm=[(u, (u + num) % upper) for u...]
    unnamed x46 -> x61, local copies, waits for them, and re-layouts: 8.85 us -> 3.07 us
    all_to_all x1 -> x0, starting transfers between devices: 5.2 us -> none  [shards(): lax.all_to_all(embed_local, 'tab', split_axis=1, concat_axis=0, tiled=True)]
  transfers between devices with their start and end apart: 4 -> 10, of which waited for: 3 -> 4; matrix products, arithmetic and copies ran while one was open for 7% -> 8% of each run, Pallas kernels for 0% -> 0%
where the time goes in v1:
time: 246 us
  waiting for transfers between devices  101 us (41%)
  blocking collectives  77.1 us (31%)
  matrix products  25.1 us (10%)
  between operations  16.1 us (7%)
  other arithmetic  9.02 us (4%)
  local copies, waits for them, and re-layouts  8.72 us (4%)
  starting transfers between devices  8.48 us (3%)
    reduce_scatter x1, waiting for transfers between devices, shards(): lax.psum_scatter(d_first_part, ('tab', 'rep'), scatter_dimension=0, tiled...  87 us
    psum x1, blocking collectives, shards(): lax.psum((part_in, part_out, part_bil, part_second, part_last), ('tab', '...  41.3 us
    all_gather x1, blocking collectives, shards(): lax.all_gather(first_all.astype(jnp.bfloat16), 'rep', axis=0, tiled=True)  14.4 us
    all_to_all x1, blocking collectives, shards(): lax.all_to_all(d_slot, 'tab', split_axis=0, concat_axis=1, tiled=True)  13.3 us
    ppermute x7, starting transfers between devices, shards(): lax.ppermute(mat_out, axis_name='tab', perm=[(u, (u + num) % upper) for u...  8.36 us
    all_gather x1, blocking collectives, shards(): all_logits = lax.all_gather(logits, 'tab', axis=0, tiled=True)  8.13 us
    psum x1, waiting for transfers between devices, shards(): lax.psum((part_in, part_out, part_bil, part_second, part_last), ('tab', '...  7.27 us
    ppermute x7, waiting for transfers between devices, shards(): lax.ppermute(mat_out, axis_name='tab', perm=[(u, (u + num) % upper) for u...  6.78 us
  transfers between devices with their start and end apart: 10, of which 4 were waited for; matrix products, arithmetic and copies ran while one was open for 8% of the time, Pallas kernels for 0%

profile of v1, /device:TPU:0, one launch (start us, length us, event | category | flops | bytes accessed | tf_op | source)
XLA Modules:
  0.0 245.6 jit_solution(17478580862682675184)
XLA Ops:
  8.1 1.0 select_reduce_fusion
  9.1 0.7 compare_and_fusion
  9.8 0.1 dynamic-slice.2
  9.9 0.1 fusion.94
  10.0 1.6 gather_fusion
  11.6 2.5 fusion.15
  14.1 0.3 fusion.52
  14.4 0.1 fusion.111
  14.5 0.5 collective-permute-start.6
  15.0 2.5 %collective-permute-start.5 = (bf16[8,128,32]{1,2,0:T(8,128)(2,1)S(1)}, bf16[8,128,32]{1,2,0:T(8,128)(2,1)S(1)}, u32[]{:S(2)}, u32[]{:S(2)}) collective-permute-start(bf16[8,128,32]{1,2,0:T(8,128)(2,1)S(1)} %get-tuple-element.22), channel_id=1, source_target_pairs={{0,8},{4,12},{8,16},{12,20},{16,24},{20,28},{24,0},{28,4},{1,9},{5... | collective-permute-start | bytes 196616 | tf_op jit(solution)/shard_map/ppermute | solution.py:126
  17.6 2.4 collective-permute-start.4
  19.9 0.5 collective-permute-start.3
  20.4 0.7 collective-permute-start
  21.1 0.6 convert_element_type.61
  21.7 0.6 reshape.133
  22.3 0.8 scatter_custom_fusion
  23.1 1.0 collective-permute-start.1
  24.0 3.9 %collective-permute-done.1 = bf16[8,128,32]{1,2,0:T(8,128)(2,1)S(1)} collective-permute-done((bf16[8,128,32]{1,2,0:T(8,128)(2,1)S(1)}, bf16[8,128,32]{1,2,0:T(8,128)(2,1)S(1)}, u32[]{:S(2)}, u32[]{:S(2)}) %collective-permute-start.1) | collective-permute-done | bytes 65568 | tf_op jit(solution)/shard_map/ppermute | solution.py:126
  27.9 0.8 collective-permute-start.2
  28.7 2.9 %collective-permute-done.2 = bf16[8,128,32]{1,2,0:T(8,128)(2,1)S(1)} collective-permute-done((bf16[8,128,32]{1,2,0:T(8,128)(2,1)S(1)}, bf16[8,128,32]{1,2,0:T(8,128)(2,1)S(1)}, u32[]{:S(2)}, u32[]{:S(2)}) %collective-permute-start.2) | collective-permute-done | bytes 65568 | tf_op jit(solution)/shard_map/ppermute | solution.py:126
  32.0 0.7 gather_fusion.1
  32.7 0.1 convert_reduce_fusion
  32.8 0.1 convolution_bitcast_fusion.3
  33.0 0.2 fusion.34
  33.2 0.2 convert_reduce_fusion.1
  33.4 1.1 fusion.9
  34.5 0.6 fusion.78
  35.2 0.4 fusion.53
  35.6 0.5 fusion.22
  36.2 0.2 copy-done.2
  36.4 0.2 copy-done.3
  36.5 0.1 copy-done.14
  36.7 0.2 multiply_convert_fusion.2
  36.9 0.8 divide_subtract_fusion
  37.7 0.2 fusion.29
  38.0 0.7 convolution_bitcast_fusion
  38.7 0.5 fusion.70
  39.3 1.5 fusion.44
  40.8 0.1 fusion.36
  40.9 0.2 fusion.30
  41.2 1.5 fusion.14
  42.7 1.4 gather_fusion.3
  44.1 13.3 %all_to_all.18 = bf16[64,128,32]{1,2,0:T(8,128)(2,1)S(1)} all-to-all(bf16[64,128,32]{1,2,0:T(8,128)(2,1)} %gather_fusion.3), channel_id=1, replica_groups=mesh['tab'=8,'rep'=4] {'tab'}, dimensions={0} | all-to-all | bytes 1048576 | tf_op jit(solution)/shard_map/all_to_all | solution.py:136
  57.4 2.8 %fusion.25 = bf16[8,128,32]{1,2,0:T(8,128)(2,1)} fusion(bf16[8,1024,128]{2,1,0:T(8,128)(2,1)} %param.12, bf16[8,128]{1,0:T(8,128)(2,1)S(1)} %copy-done.11, bf16[8,8,4,8,128]{4,3,2,1,0:T(8,128)(2,1)S(1)} %bitcast.126), kind=kOutput, calls=%fused_computation.36 | convolution fusion | flops 71335936 | bytes 2689024 | tf_op jit(solution)/shard_map/fnc,fnd->fcd/dot_general | solution.py:139
  60.3 3.8 %fusion.110 = f32[2,64,32,256]{3,2,1,0:T(8,128)} fusion(bf16[128,256,1,1]{1,0,3,2:T(8,128)(2,1)S(1)} %fusion.29, bf16[1,64,128,32]{2,3,1,0:T(8,128)(2,1)} %copy-done.3, bf16[1,64,128,32]{2,3,1,0:T(8,128)(2,1)} %copy-done.2), kind=kOutput, calls=%fused_computation.168 | convolution fusion | flops 268959744 | bytes 5308416 | tf_op jit(solution)/shard_map/kfnc,nh->kfch/dot_general | solution.py:59
  64.2 0.7 fusion.89
  64.9 8.1 %all-gather = f32[8,1,128]{2,1,0:T(1,128)S(1)} all-gather(f32[1,1,128]{2,1,0:T(1,128)S(1)} %bitcast.129), channel_id=1, replica_groups=mesh['tab'=8,'rep'=4] {'tab'}, dimensions={0}, use_global_device_ids=true | all-gather | bytes 4608 | tf_op jit(solution)/shard_map/all_gather | solution.py:149
  73.0 1.0 gather_fusion.2
  74.0 2.4 fusion.35
  76.5 1.2 and_select_fusion
  77.7 0.2 fusion.72
  77.8 0.1 fusion.90
  78.0 0.2 fusion.83
  78.2 1.0 fusion.108
  79.1 2.0 fusion.37
  81.2 41.3 %all-reduce = (f32[64,32]{0,1:T(8,128)}, f32[32,64]{1,0:T(8,128)}, f32[32,32]{1,0:T(8,128)}, f32[256]{0:T(256)}) all-reduce(f32[64,32]{0,1:T(8,128)S(1)} %fusion.72, f32[32,64]{1,0:T(8,128)S(1)} %fusion.83, f32[32,32]{1,0:T(8,128)S(1)} %fusion.37, f32[256]{0:T(256)S(1)} %bitcast.128), channel_id=1, replica_groups=mesh['tab'=8,'rep'=4] {'tab','rep'}, use_global_device_ids=true, to_apply=%region_9.10 | all-reduce | flops 5376 | bytes 43008 | tf_op jit(solution)/shard_map/psum | solution.py:146
  122.5 2.2 multiply_convert_fusion
  124.6 1.5 convert_element_type.68
  126.2 87.0 %reduce-scatter.2.cloned.1.call-done = f32[128,256]{1,0:T(8,128)} async-done(((f32[4096,256]{1,0:T(8,128)}), f32[128,256]{1,0:T(8,128)}) %reduce-scatter.2.cloned.1.call-update) | async-done | bytes 131088 | tf_op jit(solution)/shard_map/reduce_scatter | solution.py:141
  213.2 0.9 convert_element_type.69
  214.1 14.4 %all_gather.7 = bf16[512,256]{1,0:T(8,128)(2,1)S(1)} all-gather(bf16[128,256]{1,0:T(8,128)(2,1)S(1)} %convert_element_type.69), channel_id=1, replica_groups=mesh['tab'=8,'rep'=4] {'rep'}, dimensions={0}, use_global_device_ids=true | all-gather | bytes 327680 | tf_op jit(solution)/shard_map/all_gather | solution.py:142
  228.4 0.8 convert_element_type.70
  229.3 7.3 %all-reduce.6.cloned.1.call-done = f32[256,256]{1,0:T(8,128)} async-done(((f32[256,256]{1,0:T(8,128)}), f32[256,256]{1,0:T(8,128)}) %all-reduce.6.cloned.1.call-update) | async-done | bytes 262160 | tf_op jit(solution)/shard_map/psum | solution.py:146
  236.5 1.7 copy.89
  (76 shorter events, 0.6 us)
Async XLA Ops:
  8.0 27.6 %copy-start = (bf16[4096,256]{1,0:T(8,128)(2,1)S(1)}, bf16[4096,256]{1,0:T(8,128)(2,1)}, u32[]{:S(2)}) copy-start(bf16[4096,256]{1,0:T(8,128)(2,1)} %param.21) | copy-start | bytes 6291460
  8.0 116.6 %all-reduce.4.cloned.1.call-start = ((), (), s32[]{:S(2)}) async-start(), calls=%async_computation.2 | async-start | bytes 131072 | tf_op jit(solution)/shard_map/psum | solution.py:140
  9.8 4.6 %copy-start.8 = (pred[8]{0:T(512)(128)(4,1)}, pred[8]{0:T(512)(128)(4,1)S(1)}, u32[]{:S(2)}) copy-start(pred[8]{0:T(512)(128)(4,1)S(1)} %get-tuple-element.17) | copy-start | bytes 28
  10.0 4.1 %copy-start.10 = (bf16[8,128]{1,0:T(8,128)(2,1)}, bf16[8,128]{1,0:T(8,128)(2,1)S(1)}, u32[]{:S(2)}) copy-start(bf16[8,128]{1,0:T(8,128)(2,1)S(1)} %get-tuple-element.29) | copy-start | bytes 6148
  11.6 9.5 %copy-start.13 = (s32[64]{0:T(128)S(1)}, s32[64]{0:T(128)}, u32[]{:S(2)}) copy-start(s32[64]{0:T(128)} %param.14) | copy-start | bytes 772
  11.6 9.5 %copy-start.15 = (bf16[256]{0:T(256)(128)(2,1)S(1)}, bf16[256]{0:T(256)(128)(2,1)}, u32[]{:S(2)}) copy-start(bf16[256]{0:T(256)(128)(2,1)} %param.23) | copy-start | bytes 1540
  14.5 17.2 %collective-permute-start.6 = (bf16[8,128,32]{1,2,0:T(8,128)(2,1)S(1)}, bf16[8,128,32]{1,2,0:T(8,128)(2,1)S(1)}, u32[]{:S(2)}, u32[]{:S(2)}) collective-permute-start(bf16[8,128,32]{1,2,0:T(8,128)(2,1)S(1)} %get-tuple-element.21), channel_id=1, source_target_pairs={{0,4},{4,8},{8,12},{12,16},{16,20},{20,24},{24,28},{28,0},{1,5},{5... | collective-permute-start | bytes 196616 | tf_op jit(solution)/shard_map/ppermute | solution.py:126
  15.0 16.7 %collective-permute-start.5 = (bf16[8,128,32]{1,2,0:T(8,128)(2,1)S(1)}, bf16[8,128,32]{1,2,0:T(8,128)(2,1)S(1)}, u32[]{:S(2)}, u32[]{:S(2)}) collective-permute-start(bf16[8,128,32]{1,2,0:T(8,128)(2,1)S(1)} %get-tuple-element.22), channel_id=1, source_target_pairs={{0,8},{4,12},{8,16},{12,20},{16,24},{20,28},{24,0},{28,4},{1,9},{5... | collective-permute-start | bytes 196616 | tf_op jit(solution)/shard_map/ppermute | solution.py:126
  17.6 14.1 %collective-permute-start.4 = (bf16[8,128,32]{1,2,0:T(8,128)(2,1)S(1)}, bf16[8,128,32]{1,2,0:T(8,128)(2,1)S(1)}, u32[]{:S(2)}, u32[]{:S(2)}) collective-permute-start(bf16[8,128,32]{1,2,0:T(8,128)(2,1)S(1)} %get-tuple-element.23), channel_id=1, source_target_pairs={{0,12},{4,16},{8,20},{12,24},{16,28},{20,0},{24,4},{28,8},{1,13},{... | collective-permute-start | bytes 196616 | tf_op jit(solution)/shard_map/ppermute | solution.py:126
  19.9 11.7 %collective-permute-start.3 = (bf16[8,128,32]{1,2,0:T(8,128)(2,1)S(1)}, bf16[8,128,32]{1,2,0:T(8,128)(2,1)S(1)}, u32[]{:S(2)}, u32[]{:S(2)}) collective-permute-start(bf16[8,128,32]{1,2,0:T(8,128)(2,1)S(1)} %get-tuple-element.24), channel_id=1, source_target_pairs={{0,16},{4,20},{8,24},{12,28},{16,0},{20,4},{24,8},{28,12},{1,17},{... | collective-permute-start | bytes 196616 | tf_op jit(solution)/shard_map/ppermute | solution.py:126
  20.4 2.6 %collective-permute-start = (bf16[8,128,32]{1,2,0:T(8,128)(2,1)S(1)}, bf16[8,128,32]{1,2,0:T(8,128)(2,1)S(1)}, u32[]{:S(2)}, u32[]{:S(2)}) collective-permute-start(bf16[8,128,32]{1,2,0:T(8,128)(2,1)S(1)} %get-tuple-element.27), channel_id=1, source_target_pairs={{0,28},{4,0},{8,4},{12,8},{16,12},{20,16},{24,20},{28,24},{1,29},{... | collective-permute-start | bytes 196616 | tf_op jit(solution)/shard_map/ppermute | solution.py:126
  23.1 4.8 %collective-permute-start.1 = (bf16[8,128,32]{1,2,0:T(8,128)(2,1)S(1)}, bf16[8,128,32]{1,2,0:T(8,128)(2,1)S(1)}, u32[]{:S(2)}, u32[]{:S(2)}) collective-permute-start(bf16[8,128,32]{1,2,0:T(8,128)(2,1)S(1)} %get-tuple-element.26), channel_id=1, source_target_pairs={{0,24},{4,28},{8,0},{12,4},{16,8},{20,12},{24,16},{28,20},{1,25},{... | collective-permute-start | bytes 196616 | tf_op jit(solution)/shard_map/ppermute | solution.py:126
  27.9 3.7 %collective-permute-start.2 = (bf16[8,128,32]{1,2,0:T(8,128)(2,1)S(1)}, bf16[8,128,32]{1,2,0:T(8,128)(2,1)S(1)}, u32[]{:S(2)}, u32[]{:S(2)}) collective-permute-start(bf16[8,128,32]{1,2,0:T(8,128)(2,1)S(1)} %get-tuple-element.25), channel_id=1, source_target_pairs={{0,20},{4,24},{8,28},{12,0},{16,4},{20,8},{24,12},{28,16},{1,21},{... | collective-permute-start | bytes 196616 | tf_op jit(solution)/shard_map/ppermute | solution.py:126
  32.0 0.8 copy-start.5
  32.0 1.0 copy-start.6
  32.0 1.4 copy-start.4
  35.6 0.8 copy-start.2
  35.6 1.0 copy-start.3
  35.6 1.1 copy-start.14
  35.6 1.3 copy-start.12
  35.6 2.1 copy-start.16
  36.7 2.0 copy-start.18
  36.9 1.8 copy-start.20
  38.7 2.5 %copy-start.1 = (f32[2,64,128,32]{2,3,1,0:T(8,128)}, f32[2,64,128,32]{2,3,1,0:T(8,128)S(1)}, u32[]{:S(2)}) copy-start(f32[2,64,128,32]{2,3,1,0:T(8,128)S(1)} %convolution_bitcast_fusion) | copy-start | bytes 6291460
  39.2 1.5 copy-start.7
  42.7 14.7 %copy-start.11 = (bf16[8,128]{1,0:T(8,128)(2,1)S(1)}, bf16[8,128]{1,0:T(8,128)(2,1)}, u32[]{:S(2)}) copy-start(bf16[8,128]{1,0:T(8,128)(2,1)} %copy-done.10) | copy-start | bytes 6148
  60.2 152.9 %reduce-scatter.2.cloned.1.call-start = ((), (), s32[]{:S(2)}) async-start(), calls=%async_computation.3 | async-start | bytes 4325376 | tf_op jit(solution)/shard_map/reduce_scatter | solution.py:141
  64.2 14.0 %copy-start.17 = (f32[256]{0:T(256)S(1)}, f32[256]{0:T(256)}, u32[]{:S(2)}) copy-start(f32[256]{0:T(256)} %convert_element_type.61) | copy-start | bytes 3076
  64.2 172.4 %all-reduce.6.cloned.1.call-start = ((), (), s32[]{:S(2)}) async-start(), calls=%async_computation.4 | async-start | bytes 524288 | tf_op jit(solution)/shard_map/psum | solution.py:146
  74.0 4.2 %copy-start.19 = (f32[128,256]{1,0:T(8,128)S(1)}, f32[128,256]{1,0:T(8,128)}, u32[]{:S(2)}) copy-start(f32[128,256]{1,0:T(8,128)} %copy-done.18) | copy-start | bytes 393220
  74.0 4.2 %copy-start.21 = (f32[128,256]{1,0:T(8,128)S(1)}, f32[128,256]{1,0:T(8,128)}, u32[]{:S(2)}) copy-start(f32[128,256]{1,0:T(8,128)} %copy-done.20) | copy-start | bytes 393220
  76.5 46.0 %copy-start.9 = (pred[8]{0:T(512)(128)(4,1)S(1)}, pred[8]{0:T(512)(128)(4,1)}, u32[]{:S(2)}) copy-start(pred[8]{0:T(512)(128)(4,1)} %copy-done.8) | copy-start | bytes 28
Sparse Core Ops, SparseCore 0:
  60.4 37.3 all-reduce.3
  103.9 132.6 all-reduce.5
Sparse Core Ops, SparseCore 1:
  64.2 148.9 reduce-scatter.1
